TPU v7x, 128 devices: a whole 4x4x4 slice. The times are simulated.
128 devices in a mesh: dp: 32 (over x, y, core), vocab: 4 (over z).
Axes of the slice: x: 4, y: 4, z: 4, core: 2. Of those that a mesh axis runs over, the one named last changes fastest.
Arguments:
- hidden_current: bfloat16 [1024, 4096], P(('dp', 'vocab'))
- hidden_proximal: bfloat16 [1024, 4096], P(('dp', 'vocab'))
- head_current: bfloat16 [4096, 128256], P(None, ('dp', 'vocab'))
- head_proximal: bfloat16 [4096, 128256], P(None, ('dp', 'vocab'))
- targets: int32 [1024], P(('dp', 'vocab')), may hold values from 0 to 128255
- loss_mask: int32 [1024], P(('dp', 'vocab')), may hold values from 0 to 1, as said below
- lengths: int32 [128], P(('dp', 'vocab')), may hold values from 1 to 8
- behavior_logprob: float32 [1024], P(('dp', 'vocab')), may hold values from -14 to -10
- advantages: float32 [1024], P(('dp', 'vocab')), may hold values from -6 to 6
Outputs:
- token_loss: float32 [1024], P(('dp', 'vocab'))
- current_logprob: float32 [1024], P(('dp', 'vocab'))
- stats: float32 [3], replicated
Inputs may be any that keep to these rules, and one draw needn't show every extreme that they name: `loss_mask`: 1 at the first position of every sequence's window.
All inputs are finite; a program needn't handle non-finite values.
Results may differ from a plain program's by a relative error of at most 0.0003.
Values may be sent and summed in bfloat16 or wider, within the bound.
No kernel may reach another device: no remote copies, remote signals or barrier semaphores. Data moves between devices by JAX's collectives and lax.ppermute only.
A program may use at most 128 MiB of HBM per device.

v0:
```python
import jax
import jax.numpy as jnp
from jax import lax
from jax.sharding import Mesh
from jax.sharding import PartitionSpec as P

POSITIONS = 8
DP_VOCAB = ("dp_0", "dp_1", "dp_2", "vocab")
CLIP_EPS = 0.2
WEIGHT_CAP = 5.0


def joined_along(blocks, dim):
    lengths = list(blocks.shape[1:])
    lengths[dim] *= blocks.shape[0]
    return jnp.moveaxis(blocks, 0, dim).reshape(lengths)


def gather_in_order(x, axes, turns):
    blocks = x
    for k in turns:
        blocks = lax.all_gather(blocks, axes[k])
    done = turns[::-1]
    back = [done.index(k) for k in range(len(axes))]
    blocks = blocks.transpose(*back, *range(len(axes), blocks.ndim))
    return blocks.reshape(-1, *x.shape)


def gather_axes(x, axes, turns, dim):
    return joined_along(gather_in_order(x, axes, turns), dim)


def rows_first(arrays, axis, dims):
    turned = [jnp.moveaxis(a, dim, 0) for a, dim in zip(arrays, dims)]
    widths = [t[0].size for t in turned]
    both = jnp.concatenate([t.reshape(-1, w) for t, w in zip(turned, widths)], axis=1)
    result = lax.all_gather(both, axis, axis=0, tiled=True)
    blocks = jnp.split(result, [sum(widths[:k]) for k in range(1, len(widths))], axis=1)
    return tuple(
        (
            jnp.moveaxis(b.reshape(-1, *t.shape[1:]), 0, dim)
            for b, t, dim in zip(blocks, turned, dims)
        )
    )


def all_in_one(x, axis):
    leaves = jax.tree.leaves(x)
    turns = sorted(range(len(leaves)), key=lambda k: -leaves[k].size)
    width = (1, *leaves[turns[0]].shape)[-1]
    lines = [
        jnp.pad(leaves[k].reshape(-1), (0, -leaves[k].size % width)).reshape(-1, width)
        for k in turns
    ]
    both, at, found = (lax.all_gather(jnp.concatenate(lines), axis), 0, {})
    for k, line in zip(turns, lines):
        piece = both[:, at : at + len(line)].reshape(len(both), -1)
        found[k] = piece[:, : leaves[k].size].reshape(-1, *leaves[k].shape)
        at += len(line)
    numbers = iter(range(len(leaves)))
    return jax.tree.map(lambda _: found[next(numbers)], x)


def combined_by_axis(x, axes, combine):
    for axis in axes:
        pieces = all_in_one(x, axis)
        x = jax.tree.map(lambda part: part[0], pieces)
        for k in range(1, lax.axis_size(axis)):
            x = combine(x, jax.tree.map(lambda part: part[k], pieces))
    return x


def column_stats(logits, wanted, first_col, with_entropy):
    peak = jnp.max(logits, axis=1)
    weights = jnp.exp(logits - peak[:, None])
    total = jnp.sum(weights, axis=1)
    columns = first_col + lax.broadcasted_iota(jnp.int32, logits.shape, 1)
    picked = jnp.sum(jnp.where(columns == wanted[:, None], logits, jnp.float32(0.0)), axis=1)
    if with_entropy:
        moment = jnp.sum(weights * logits, axis=1)
        return [peak, total, moment, picked]
    return [peak, total, picked]


def token_terms(logp_current, logp_proximal, entropy, advantages, behavior, live):
    ratio = jnp.exp(logp_current - logp_proximal)
    clipped = jnp.clip(ratio, 1.0 - CLIP_EPS, 1.0 + CLIP_EPS)
    surrogate = jnp.maximum(-advantages * ratio, -advantages * clipped)
    weight = jnp.minimum(jnp.exp(logp_proximal - behavior), WEIGHT_CAP)
    return (surrogate * weight * live, weight * live, entropy * live)


def merge_rows(first, second):
    peak_c = jnp.maximum(first[0], second[0])
    fa_c = jnp.exp(first[0] - peak_c)
    fb_c = jnp.exp(second[0] - peak_c)
    peak_p = jnp.maximum(first[4], second[4])
    fa_p = jnp.exp(first[4] - peak_p)
    fb_p = jnp.exp(second[4] - peak_p)
    return (
        peak_c,
        first[1] * fa_c + second[1] * fb_c,
        first[2] * fa_c + second[2] * fb_c,
        first[3] + second[3],
        peak_p,
        first[5] * fa_p + second[5] * fb_p,
        first[6] + second[6],
    )


def local(
    hidden_current,
    hidden_proximal,
    head_current,
    head_proximal,
    targets,
    loss_mask,
    lengths,
    behavior_logprob,
    advantages,
):
    tok_dev = targets.shape[0]
    first_col = lax.axis_index(DP_VOCAB) * head_current.shape[1]
    row_start = lax.axis_index(DP_VOCAB) * tok_dev
    all_targets = gather_axes(targets, DP_VOCAB, (0, 1, 3, 2), 0)
    place = lax.broadcasted_iota(jnp.int32, (lengths.shape[0], POSITIONS), 1)
    live = ((place < lengths[:, None]).reshape(-1) & (loss_mask == 1)).astype(jnp.float32)
    spread_adv, spread_behav, spread_live = rows_first(
        (advantages, behavior_logprob, live), DP_VOCAB, (0, 0, 0)
    )
    stacked = jnp.stack([hidden_current, hidden_proximal])
    pieces = lax.all_gather(stacked, DP_VOCAB, axis=1, tiled=True)
    logits = jnp.dot(pieces[0], head_current, preferred_element_type=jnp.float32)
    proximal_logits = jnp.dot(pieces[1], head_proximal, preferred_element_type=jnp.float32)
    stats = jnp.concatenate(
        [
            jnp.stack(column_stats(logits, all_targets, first_col, True)),
            jnp.stack(column_stats(proximal_logits, all_targets, first_col, False)),
        ],
        axis=0,
    )
    peak_c, total_c, moment_c, picked_c, peak_p, total_p, picked_p = combined_by_axis(
        (stats[0], stats[1], stats[2], stats[3], stats[4], stats[5], stats[6]), DP_VOCAB, merge_rows
    )
    lse_c = peak_c + jnp.log(total_c)
    logp_c = picked_c - lse_c
    entropy = lse_c - moment_c / total_c
    logp_p = picked_p - (peak_p + jnp.log(total_p))

    def mine(values):
        return lax.dynamic_slice_in_dim(values, row_start, tok_dev)

    loss_all, weight_all, ent_all = token_terms(
        logp_c, logp_p, entropy, spread_adv, spread_behav, spread_live
    )
    loss_sum = jnp.sum(loss_all)
    weight_sum = jnp.sum(weight_all)
    ent_sum = jnp.sum(ent_all)
    count = jnp.sum(spread_live)
    token_loss = mine(loss_all)
    summary = jnp.stack([loss_sum / count, weight_sum / count, ent_sum / count])
    return (token_loss, mine(logp_c), summary)


def solution(mesh):
    torus = Mesh(
        mesh.devices.reshape(4, 4, 2, mesh.shape["vocab"]), ("dp_0", "dp_1", "dp_2", "vocab")
    )
    return jax.shard_map(
        local,
        mesh=torus,
        in_specs=(
            P(DP_VOCAB, None),
            P(DP_VOCAB, None),
            P(None, DP_VOCAB),
            P(None, DP_VOCAB),
            P(DP_VOCAB),
            P(DP_VOCAB),
            P(DP_VOCAB),
            P(DP_VOCAB),
            P(DP_VOCAB),
        ),
        out_specs=(P(DP_VOCAB), P(DP_VOCAB), P()),
        check_vma=False,
    )
```

profile of v0, /device:TPU:0, one launch (start us, length us, event | category | flops | bytes accessed | tf_op | source)
XLA Modules:
  0.0 191.8 jit_solution(17642314294990038285)
XLA Ops:
  7.2 1.5 pad_maximum_fusion
  8.8 1.2 dynamic-slice
  10.7 0.9 dynamic-update-slice
  11.5 9.0 %all-reduce = s32[32]{0:T(128)S(1)} all-reduce(s32[32]{0:T(128)S(1)} %dynamic-update-slice), channel_id=2, replica_groups=mesh['dp_0'=4,'dp_1'=4,'dp_2'=2,'vocab'=4] {'dp_0'}, use_global_device_ids=true, to_apply=%add | all-reduce | flops 32 | bytes 256
  20.6 11.3 %all-gather.9 = s32[4,4,8]{2,1,0:T(4,128)S(1)} all-gather(s32[1,4,8]{2,1,0:T(4,128)S(1)} %reshape.1551), channel_id=3, replica_groups=mesh['dp_0'=4,'dp_1'=4,'dp_2'=2,'vocab'=4] {'dp_1'}, dimensions={0}, use_global_device_ids=true | all-gather | bytes 640 | tf_op jit(solution)/shard_map/all_gather | solution.py:22
  31.9 13.1 %all-gather.2 = s32[16,4,8]{2,1,0:T(4,128)S(1)} all-gather(s32[4,4,8]{2,1,0:T(4,128)S(1)} %all-gather.9), channel_id=4, replica_groups=mesh['dp_0'=4,'dp_1'=4,'dp_2'=2,'vocab'=4] {'vocab'}, dimensions={0}, use_global_device_ids=true | all-gather | bytes 2560 | tf_op jit(solution)/shard_map/all_gather | solution.py:22
  45.0 1.8 all-gather.3
  47.7 0.7 fusion.95
  48.3 0.7 maximum_bitcast_fusion
  49.0 61.3 %all-gather.8 = f32[128,8,3]{1,2,0:T(4,128)S(1)} all-gather(f32[1,8,3]{1,2,0:T(4,128)S(1)} %maximum_bitcast_fusion), channel_id=1, replica_groups=mesh['dp_0'=4,'dp_1'=4,'dp_2'=2,'vocab'=4] {'dp_0','dp_1','dp_2','vocab'}, dimensions={0}, use_global_device_ids=true | all-gather | bytes 12384 | tf_op jit(solution)/shard_map/all_gather | solution.py:37
  110.3 0.1 reshape.1550
  110.5 0.6 slice_reduce_fusion
  111.1 12.8 %fusion.106 = (f32[1024]{0:T(1024)S(1)}, f32[1024,1002]{0,1:T(8,128)S(1)}) fusion(bf16[4096,1002]{0,1:T(8,128)(2,1)} %param.11, bf16[2,1024,4096]{2,1,0:T(8,128)(2,1)} %all-gather.16.cloned.1.call-done), kind=kOutput, calls=%fused_computation.216 | convolution fusion | flops 8406410240 | bytes 20754432 | tf_op jit(solution)/shard_map/dot_general | solution.py:133
  123.9 12.8 %fusion.107 = (f32[1024]{0:T(1024)S(1)}, f32[1024,1002]{0,1:T(8,128)S(1)}) fusion(bf16[4096,1002]{0,1:T(8,128)(2,1)} %param.12, bf16[2,1024,4096]{2,1,0:T(8,128)(2,1)} %all-gather.16.cloned.1.call-done), kind=kOutput, calls=%fused_computation.217 | convolution fusion | flops 8406410240 | bytes 20754432 | tf_op jit(solution)/shard_map/dot_general | solution.py:134
  136.7 2.5 %fusion.3 = (f32[1024]{0:T(1024)S(1)}, f32[1024]{0:T(1024)S(1)}, f32[1024]{0:T(1024)S(1)}, f32[1024]{0:T(1024)S(1)}, f32[1024]{0:T(1024)S(1)}) fusion(f32[1024,1002]{0,1:T(8,128)S(1)} %get-tuple-element.69, s32[1024]{0:T(1024)S(1)} %eq.18, s32[1002]{0:T(1024)S(1)} %iota_add_fusion, f32[1024]{0:T(1024)S(1)} %get-tuple-element.68, ...), kind=kLoop, calls=%fused_computation.7 | loop fusion | flops 11281408 | bytes 8245160 | tf_op jit(solution)/shard_map/reduce_sum | solution.py:78
  139.3 12.0 %all-gather.10 = f32[4,7,1024]{2,1,0:T(8,128)S(1)} all-gather(f32[1,7,1024]{2,1,0:T(8,128)S(1)} %bitcast.552), channel_id=6, replica_groups=mesh['dp_0'=4,'dp_1'=4,'dp_2'=2,'vocab'=4] {'dp_0'}, dimensions={0}, use_global_device_ids=true | all-gather | bytes 143360 | tf_op jit(solution)/shard_map/all_gather | solution.py:55
  151.5 12.0 %all-gather.11 = f32[4,7,1024]{2,1,0:T(8,128)S(1)} all-gather(f32[1,7,1024]{2,1,0:T(8,128)S(1)} %bitcast.553), channel_id=7, replica_groups=mesh['dp_0'=4,'dp_1'=4,'dp_2'=2,'vocab'=4] {'dp_1'}, dimensions={0}, use_global_device_ids=true | all-gather | bytes 143360 | tf_op jit(solution)/shard_map/all_gather | solution.py:55
  163.8 1.9 all-gather.12
  165.8 12.0 %all-gather.13 = f32[4,7,1024]{2,1,0:T(8,128)S(1)} all-gather(f32[1,7,1024]{2,1,0:T(8,128)S(1)} %bitcast.555), channel_id=9, replica_groups=mesh['dp_0'=4,'dp_1'=4,'dp_2'=2,'vocab'=4] {'vocab'}, dimensions={0}, use_global_device_ids=true | all-gather | bytes 143360 | tf_op jit(solution)/shard_map/all_gather | solution.py:55
  177.9 0.6 fusion.96
  179.9 0.6 multiply_reduce_fusion.2
  183.2 0.6 dynamic_slice.7
  183.8 0.6 dynamic_slice.6
  184.4 0.6 pad_maximum_fusion.1
  (24 shorter events, 1.0 us)
Async XLA Ops:
  7.2 103.9 %all-gather.16.cloned.1.call-start = ((), (), s32[]{:S(2)}) async-start(), calls=%async_computation | async-start | bytes 16908288 | tf_op jit(solution)/shard_map/all_gather | solution.py:132
Sparse Core Ops, SparseCore 0:
  11.0 83.1 all-gather.15
where the time goes:
time: 192 us
  blocking collectives  134 us (70%)
  matrix products  25.6 us (13%)
  between operations  19.5 us (10%)
  other arithmetic  8.41 us (4%)
  local copies, waits for them, and re-layouts  3.87 us (2%)
    all_gather x1, blocking collectives, rows_first(): result = lax.all_gather(both, axis, axis=0, tiled=True)  61.3 us
    all_gather x4, blocking collectives, all_in_one(): both, at, found = (lax.all_gather(jnp.concatenate(lines), axis), 0, {})  37.8 us
    all_gather x3, blocking collectives, gather_in_order(): blocks = lax.all_gather(blocks, axes[k])  26.3 us
    dot_general x1, matrix products, local(): jnp.dot(pieces[1], head_proximal, preferred_element_type=jnp.float32)  12.8 us
    dot_general x1, matrix products, local(): jnp.dot(pieces[0], head_current, preferred_element_type=jnp.float32)  12.8 us
    unnamed x1, blocking collectives  8.99 us
  transfers between devices with their start and end apart: 1, of which 0 were waited for; matrix products, arithmetic and copies ran while one was open for 2% of the time, Pallas kernels for 0%

commit v1 on v0

--- a/solution.py
+++ b/solution.py
@@ -34,7 +34,9 @@
     turned = [jnp.moveaxis(a, dim, 0) for a, dim in zip(arrays, dims)]
     widths = [t[0].size for t in turned]
     both = jnp.concatenate([t.reshape(-1, w) for t, w in zip(turned, widths)], axis=1)
-    result = lax.all_gather(both, axis, axis=0, tiled=True)
+    result = jnp.concatenate(
+        lax.all_to_all(jnp.stack([both] * lax.axis_size(axis)), axis, 0, 0), axis=0
+    )
     blocks = jnp.split(result, [sum(widths[:k]) for k in range(1, len(widths))], axis=1)
     return tuple(
         (

time: 192 us -> 176 us (0.917)
  blocking collectives: 134 us -> 72.8 us
  waiting for transfers between devices: 0.02 us -> 33.8 us
  starting transfers between devices: 0.04 us -> 11.2 us
    all_gather x1 -> x0, blocking collectives: 61.3 us -> none  [rows_first(): result = lax.all_gather(both, axis, axis=0, tiled=True)]
    all_gather x1, waiting for transfers between devices: 0.01 us -> 33.7 us  [local(): pieces = lax.all_gather(stacked, DP_VOCAB, axis=1, tiled=True)]
    all_to_all x0 -> x1, starting transfers between devices: none -> 11.2 us  [rows_first(): lax.all_to_all(jnp.stack([both] * lax.axis_size(axis)), axis, 0, 0)]
  transfers between devices with their start and end apart: 1 -> 2, of which waited for: 0 -> 1; matrix products, arithmetic and copies ran while one was open for 2% -> 3% of each run, Pallas kernels for 0% -> 0%
where the time goes in v1:
time: 176 us
  blocking collectives  72.8 us (41%)
  waiting for transfers between devices  33.8 us (19%)
  matrix products  25.6 us (15%)
  between operations  19.5 us (11%)
  starting transfers between devices  11.2 us (6%)
  other arithmetic  8.43 us (5%)
  local copies, waits for them, and re-layouts  4.61 us (3%)
    all_gather x4, blocking collectives, all_in_one(): both, at, found = (lax.all_gather(jnp.concatenate(lines), axis), 0, {})  38.7 us
    all_gather x1, waiting for transfers between devices, local(): pieces = lax.all_gather(stacked, DP_VOCAB, axis=1, tiled=True)  33.7 us
    all_gather x3, blocking collectives, gather_in_order(): blocks = lax.all_gather(blocks, axes[k])  25.7 us
    dot_general x1, matrix products, local(): jnp.dot(pieces[1], head_proximal, preferred_element_type=jnp.float32)  12.8 us
    dot_general x1, matrix products, local(): jnp.dot(pieces[0], head_current, preferred_element_type=jnp.float32)  12.8 us
    all_to_all x1, starting transfers between devices, rows_first(): lax.all_to_all(jnp.stack([both] * lax.axis_size(axis)), axis, 0, 0)  11.2 us
    unnamed x1, blocking collectives  8.32 us
  transfers between devices with their start and end apart: 2, of which 1 were waited for; matrix products, arithmetic and copies ran while one was open for 3% of the time, Pallas kernels for 0%

profile of v1, /device:TPU:0, one launch (start us, length us, event | category | flops | bytes accessed | tf_op | source)
XLA Modules:
  0.0 175.9 jit_solution(18194553068011569381)
XLA Ops:
  7.2 1.5 pad_maximum_fusion
  9.4 0.7 fusion.95
  10.1 0.7 pad_maximum_fusion.1
  10.8 0.7 stack.16
  11.5 11.2 %all-to-all-start = ((f32[128,8,3]{1,2,0:T(4,128)}), f32[128,8,3]{1,2,0:T(4,128)S(1)}, u32[]{:S(2)}, u32[]{:S(2)}) async-start(f32[128,8,3]{1,2,0:T(4,128)} %stack.16), calls=%async_computation | async-start | bytes 524288 | tf_op jit(solution)/shard_map/all_to_all | solution.py:38
  22.7 1.2 dynamic-slice
  24.6 0.9 dynamic-update-slice
  25.5 8.3 %all-reduce = s32[32]{0:T(128)S(1)} all-reduce(s32[32]{0:T(128)S(1)} %dynamic-update-slice), channel_id=2, replica_groups=mesh['dp_0'=4,'dp_1'=4,'dp_2'=2,'vocab'=4] {'dp_0'}, use_global_device_ids=true, to_apply=%add | all-reduce | flops 32 | bytes 256
  33.9 11.1 %all-gather.8 = s32[4,4,8]{2,1,0:T(4,128)S(1)} all-gather(s32[1,4,8]{2,1,0:T(4,128)S(1)} %reshape.1555), channel_id=3, replica_groups=mesh['dp_0'=4,'dp_1'=4,'dp_2'=2,'vocab'=4] {'dp_1'}, dimensions={0}, use_global_device_ids=true | all-gather | bytes 640 | tf_op jit(solution)/shard_map/all_gather | solution.py:22
  45.0 12.7 %all-gather.2 = s32[16,4,8]{2,1,0:T(4,128)S(1)} all-gather(s32[4,4,8]{2,1,0:T(4,128)S(1)} %all-gather.8), channel_id=4, replica_groups=mesh['dp_0'=4,'dp_1'=4,'dp_2'=2,'vocab'=4] {'vocab'}, dimensions={0}, use_global_device_ids=true | all-gather | bytes 2560 | tf_op jit(solution)/shard_map/all_gather | solution.py:22
  57.7 1.8 %all-gather.3 = s32[8,4,4,8]{3,2,1,0:T(4,128)S(1)} all-gather(s32[4,4,4,8]{3,2,1,0:T(4,128)S(1)} %bitcast.549), channel_id=5, replica_groups=mesh['dp_0'=4,'dp_1'=4,'dp_2'=2,'vocab'=4] {'dp_2'}, dimensions={0}, use_global_device_ids=true | all-gather | bytes 6144 | tf_op jit(solution)/shard_map/all_gather | solution.py:22
  59.9 0.6 slice_reduce_fusion
  60.5 33.7 %all-gather.15.cloned.1.call-done = bf16[2,1024,4096]{2,1,0:T(8,128)(2,1)} async-done(((bf16[2,8,4096]{2,1,0:T(8,128)(2,1)}), bf16[2,1024,4096]{2,1,0:T(8,128)(2,1)}) %all-gather.15.cloned.1.call-update) | async-done | bytes 16777232 | tf_op jit(solution)/shard_map/all_gather | solution.py:134
  94.3 12.8 %fusion.106 = (f32[1024]{0:T(1024)S(1)}, f32[1024,1002]{0,1:T(8,128)S(1)}) fusion(bf16[4096,1002]{0,1:T(8,128)(2,1)} %param.11, bf16[2,1024,4096]{2,1,0:T(8,128)(2,1)} %all-gather.15.cloned.1.call-done), kind=kOutput, calls=%fused_computation.216 | convolution fusion | flops 8406410240 | bytes 20754432 | tf_op jit(solution)/shard_map/dot_general | solution.py:135
  107.1 12.8 %fusion.107 = (f32[1024]{0:T(1024)S(1)}, f32[1024,1002]{0,1:T(8,128)S(1)}) fusion(bf16[4096,1002]{0,1:T(8,128)(2,1)} %param.12, bf16[2,1024,4096]{2,1,0:T(8,128)(2,1)} %all-gather.15.cloned.1.call-done), kind=kOutput, calls=%fused_computation.217 | convolution fusion | flops 8406410240 | bytes 20754432 | tf_op jit(solution)/shard_map/dot_general | solution.py:136
  119.9 2.5 %fusion.3 = (f32[1024]{0:T(1024)S(1)}, f32[1024]{0:T(1024)S(1)}, f32[1024]{0:T(1024)S(1)}, f32[1024]{0:T(1024)S(1)}, f32[1024]{0:T(1024)S(1)}) fusion(f32[1024,1002]{0,1:T(8,128)S(1)} %get-tuple-element.69, s32[1024]{0:T(1024)S(1)} %eq.18, s32[1002]{0:T(1024)S(1)} %iota_add_fusion, f32[1024]{0:T(1024)S(1)} %get-tuple-element.68, ...), kind=kLoop, calls=%fused_computation.7 | loop fusion | flops 11281408 | bytes 8245160 | tf_op jit(solution)/shard_map/reduce_sum | solution.py:80
  122.5 12.3 %all-gather.9 = f32[4,7,1024]{2,1,0:T(8,128)S(1)} all-gather(f32[1,7,1024]{2,1,0:T(8,128)S(1)} %bitcast.550), channel_id=6, replica_groups=mesh['dp_0'=4,'dp_1'=4,'dp_2'=2,'vocab'=4] {'dp_0'}, dimensions={0}, use_global_device_ids=true | all-gather | bytes 143360 | tf_op jit(solution)/shard_map/all_gather | solution.py:57
  135.0 12.5 %all-gather.10 = f32[4,7,1024]{2,1,0:T(8,128)S(1)} all-gather(f32[1,7,1024]{2,1,0:T(8,128)S(1)} %bitcast.551), channel_id=7, replica_groups=mesh['dp_0'=4,'dp_1'=4,'dp_2'=2,'vocab'=4] {'dp_1'}, dimensions={0}, use_global_device_ids=true | all-gather | bytes 143360 | tf_op jit(solution)/shard_map/all_gather | solution.py:57
  147.7 1.9 %all-gather.11 = f32[2,7,1024]{2,1,0:T(8,128)S(1)} all-gather(f32[1,7,1024]{2,1,0:T(8,128)S(1)} %bitcast.552), channel_id=8, replica_groups=mesh['dp_0'=4,'dp_1'=4,'dp_2'=2,'vocab'=4] {'dp_2'}, dimensions={0}, use_global_device_ids=true | all-gather | bytes 86016 | tf_op jit(solution)/shard_map/all_gather | solution.py:57
  149.7 12.1 %all-gather.12 = f32[4,7,1024]{2,1,0:T(8,128)S(1)} all-gather(f32[1,7,1024]{2,1,0:T(8,128)S(1)} %bitcast.553), channel_id=9, replica_groups=mesh['dp_0'=4,'dp_1'=4,'dp_2'=2,'vocab'=4] {'vocab'}, dimensions={0}, use_global_device_ids=true | all-gather | bytes 143360 | tf_op jit(solution)/shard_map/all_gather | solution.py:57
  162.0 0.6 fusion.96
  164.0 0.6 multiply_reduce_fusion.2
  167.3 0.6 dynamic_slice.7
  168.4 0.6 pad_maximum_fusion.2
  (26 shorter events, 1.8 us)
Async XLA Ops:
  7.2 87.1 %all-gather.15.cloned.1.call-start = ((), (), s32[]{:S(2)}) async-start(), calls=%async_computation.1 | async-start | bytes 16908288 | tf_op jit(solution)/shard_map/all_gather | solution.py:134
  11.5 48.2 %all-to-all-start = ((f32[128,8,3]{1,2,0:T(4,128)}), f32[128,8,3]{1,2,0:T(4,128)S(1)}, u32[]{:S(2)}, u32[]{:S(2)}) async-start(f32[128,8,3]{1,2,0:T(4,128)} %stack.16), calls=%async_computation | async-start | bytes 524288 | tf_op jit(solution)/shard_map/all_to_all | solution.py:38
Sparse Core Ops, SparseCore 0:
  11.0 83.2 all-gather.14
